TPU v7x, 32 devices: a whole 2x2x4 slice. The times are simulated.
32 devices in a mesh: rep: 16 (over z, x, core), tp: 2 (over y).
Axes of the slice: x: 2, y: 2, z: 4, core: 2. Of those that a mesh axis runs over, the one named last changes fastest.
Arguments:
- tokens: bfloat16 [16, 256, 3072], P('rep', 'tp'), may hold values from -100 to 100
- norm_gain: float32 [16, 3072], P('rep'), may hold values from 0.5 to 1.5
- w_query: bfloat16 [16, 3072, 2048], P('rep', None, 'tp'), may hold values from -1 to 1
- key_weight: bfloat16 [16, 3072, 1024], P('rep', None, 'tp'), may hold values from -1 to 1
- value_weight: bfloat16 [16, 3072, 1024], P('rep', None, 'tp'), may hold values from -0.109375 to 0.109375
- attention_gradient: bfloat16 [16, 256, 2048], P('rep', None, 'tp'), may hold values from -6 to 6
- global_fragment: float32 [128, 3072], P('tp'), may hold values from -6 to 6
- momentum: float32 [128, 3072], P('tp'), may hold values from -3 to 3
- local_fragment: bfloat16 [16, 128, 3072], P('rep', 'tp'), may hold values from -6 to 6
Outputs:
- grad_query_w: bfloat16 [16, 3072, 2048], P('rep', None, 'tp')
- grad_key_w: bfloat16 [16, 3072, 1024], P('rep', None, 'tp')
- grad_value_w: bfloat16 [16, 3072, 1024], P('rep', None, 'tp')
- grad_gain: float32 [16, 3072], P('rep')
- grad_tokens: bfloat16 [16, 256, 3072], P('rep', 'tp')
- new_global: float32 [128, 3072], P('tp')
- new_momentum: float32 [128, 3072], P('tp')
All inputs are finite; a program needn't handle non-finite values.
Results may differ from a plain program's by a relative error of at most 0.019.
The roundings to bfloat16 on the way count: a program that leaves them out, or rounds other values in their place, can miss the bound.
Values may be sent and summed in bfloat16 or wider, within the bound.
A program may use at most 128 MiB of HBM per device.

v0:
```python
import jax
import jax.numpy as jnp
from jax import lax
from jax.sharding import PartitionSpec as P

HEAD_SIZE = 128
epsilon = 1e-05
rope_base = 500000.0
outer_rate = 0.7
outer_momentum = 0.9


def rope_tables(sequence_length, width):
    middle = width // 2
    frequency = rope_base ** (-2.0 * jnp.arange(middle, dtype=jnp.float32) / width)
    angles = jnp.arange(sequence_length, dtype=jnp.float32)[:, None] * frequency[None, :]
    angles = jnp.concatenate([angles, angles], axis=1)
    return (jnp.cos(angles)[:, None, :], jnp.sin(angles)[:, None, :])


def rotate(vectors, cosine_table, sine_table):
    middle = vectors.shape[-1] // 2
    turned = jnp.concatenate([-vectors[..., middle:], vectors[..., :middle]], axis=-1)
    return vectors * cosine_table + turned * sine_table


def reverse_rotation(gradient, cosine_table, sine_table):
    middle = gradient.shape[-1] // 2
    shifted = gradient * sine_table
    turned = jnp.concatenate([shifted[..., middle:], -shifted[..., :middle]], axis=-1)
    return gradient * cosine_table + turned


def attention_reverse(query_rows, rotated_keys, values_bfloat, grad_out, block_of_rows):
    sequence_length = query_rows.shape[0]
    score_scale = query_rows.shape[-1] ** (-0.5)

    def one_block(running, block_index):
        acc_key, acc_value = running
        offset = block_index * block_of_rows
        query_block = lax.dynamic_slice_in_dim(query_rows, offset, block_of_rows, 0)
        grad_block = lax.dynamic_slice_in_dim(grad_out, offset, block_of_rows, 0)
        scores = (
            jnp.einsum(
                "qgrd,kgd->grqk", query_block, rotated_keys, preferred_element_type=jnp.float32
            )
            * score_scale
        )
        row_pos = offset + jnp.arange(block_of_rows)
        col_pos = jnp.arange(sequence_length)
        allowed = col_pos[None, :] <= row_pos[:, None]
        scores = jnp.where(allowed, scores, -jnp.inf)
        highest = jnp.max(scores, axis=-1, keepdims=True)
        powers = jnp.exp(scores - highest)
        probability = powers / jnp.sum(powers, axis=-1, keepdims=True)
        prob_low = probability.astype(jnp.bfloat16)
        acc_value = acc_value + jnp.einsum(
            "grqk,qgrd->kgd", prob_low, grad_block, preferred_element_type=jnp.float32
        )
        grad_prob = jnp.einsum(
            "qgrd,kgd->grqk", grad_block, values_bfloat, preferred_element_type=jnp.float32
        )
        grad_score = (
            probability
            * (grad_prob - jnp.sum(grad_prob * probability, axis=-1, keepdims=True))
            * score_scale
        )
        score_low = grad_score.astype(jnp.bfloat16)
        grad_query = jnp.einsum(
            "grqk,kgd->qgrd", score_low, rotated_keys, preferred_element_type=jnp.float32
        )
        acc_key = acc_key + jnp.einsum(
            "grqk,qgrd->kgd", score_low, query_block, preferred_element_type=jnp.float32
        )
        return ((acc_key, acc_value), grad_query)

    initial = jnp.zeros(rotated_keys.shape, jnp.float32)
    (acc_key, acc_value), grad_blocks = lax.scan(
        one_block, (initial, initial), jnp.arange(sequence_length // block_of_rows)
    )
    return (grad_blocks.reshape(query_rows.shape), acc_key, acc_value)


def body(
    tokens,
    norm_gain,
    w_query,
    key_weight,
    value_weight,
    attention_gradient,
    global_fragment,
    momentum,
    local_fragment,
):
    local_rows = tokens[0]
    norm_gains = norm_gain[0]
    weight_q = w_query[0]
    weight_k = key_weight[0]
    weight_v = value_weight[0]
    widened_rows = local_rows.astype(jnp.float32)
    inverse_norm = lax.rsqrt(
        jnp.mean(widened_rows * widened_rows, axis=-1, keepdims=True) + epsilon
    )
    normalized_input = widened_rows * inverse_norm
    normalized_local = (normalized_input * norm_gains[None, :]).astype(jnp.bfloat16)
    normalized = lax.all_gather(normalized_local, "tp", axis=0, tiled=True)
    sequence_length = normalized.shape[0]
    heads_q = weight_q.shape[1] // HEAD_SIZE
    heads_kv = weight_k.shape[1] // HEAD_SIZE
    cosine_table, sine_table = rope_tables(sequence_length, HEAD_SIZE)
    query_rows = jnp.dot(normalized, weight_q, preferred_element_type=jnp.float32).reshape(
        sequence_length, heads_q, HEAD_SIZE
    )
    query_rows = rotate(query_rows, cosine_table, sine_table).astype(jnp.bfloat16)
    rotated_keys = jnp.dot(normalized, weight_k, preferred_element_type=jnp.float32).reshape(
        sequence_length, heads_kv, HEAD_SIZE
    )
    rotated_keys = rotate(rotated_keys, cosine_table, sine_table).astype(jnp.bfloat16)
    values_bfloat = (
        jnp.dot(normalized, weight_v, preferred_element_type=jnp.float32)
        .astype(jnp.bfloat16)
        .reshape(sequence_length, heads_kv, HEAD_SIZE)
    )
    replica_group = heads_q // heads_kv
    block_of_rows = min(512, sequence_length)
    query_input_gradient, key_input_gradient, value_input_gradient = attention_reverse(
        query_rows.reshape(sequence_length, heads_kv, replica_group, HEAD_SIZE),
        rotated_keys,
        values_bfloat,
        attention_gradient[0].reshape(sequence_length, heads_kv, replica_group, HEAD_SIZE),
        block_of_rows,
    )
    dquery = (
        reverse_rotation(
            query_input_gradient.reshape(sequence_length, heads_q, HEAD_SIZE),
            cosine_table,
            sine_table,
        )
        .astype(jnp.bfloat16)
        .reshape(sequence_length, heads_q * HEAD_SIZE)
    )
    key_gradient = (
        reverse_rotation(key_input_gradient, cosine_table, sine_table)
        .astype(jnp.bfloat16)
        .reshape(sequence_length, heads_kv * HEAD_SIZE)
    )
    value_gradient = value_input_gradient.astype(jnp.bfloat16).reshape(
        sequence_length, heads_kv * HEAD_SIZE
    )
    contract = (((0,), (0,)), ((), ()))
    grad_wq = lax.dot_general(
        normalized, dquery, contract, preferred_element_type=jnp.float32
    ).astype(jnp.bfloat16)
    grad_wk = lax.dot_general(
        normalized, key_gradient, contract, preferred_element_type=jnp.float32
    ).astype(jnp.bfloat16)
    grad_wv = lax.dot_general(
        normalized, value_gradient, contract, preferred_element_type=jnp.float32
    ).astype(jnp.bfloat16)
    back = (((1,), (1,)), ((), ()))
    partial_value = lax.dot_general(dquery, weight_q, back, preferred_element_type=jnp.float32)
    partial_value = partial_value + lax.dot_general(
        key_gradient, weight_k, back, preferred_element_type=jnp.float32
    )
    summed_rows = lax.psum_scatter(
        (
            partial_value
            + lax.dot_general(value_gradient, weight_v, back, preferred_element_type=jnp.float32)
        ).astype(jnp.bfloat16),
        "tp",
        scatter_dimension=0,
        tiled=True,
    ).astype(jnp.float32)
    gains_gradient = lax.psum(jnp.sum(summed_rows * normalized_input, axis=0), "tp")
    scaled_rows = summed_rows * norm_gains[None, :]
    gradient_rows = (
        inverse_norm
        * (
            scaled_rows
            - normalized_input * jnp.mean(scaled_rows * normalized_input, axis=-1, keepdims=True)
        )
    ).astype(jnp.bfloat16)
    delta = global_fragment - local_fragment[0].astype(jnp.float32)
    replicas = lax.axis_size("rep")
    mean_delta = lax.psum(delta, "rep") / replicas
    new_momentum = outer_momentum * momentum + mean_delta
    new_global = global_fragment - outer_rate * (mean_delta + outer_momentum * new_momentum)
    return (
        grad_wq[None],
        grad_wk[None],
        grad_wv[None],
        gains_gradient[None],
        gradient_rows[None],
        new_global,
        new_momentum,
    )


def solution(mesh):
    placed = (
        P("rep", "tp", None),
        P("rep", None),
        P("rep", None, "tp"),
        P("rep", None, "tp"),
        P("rep", None, "tp"),
        P("rep", None, "tp"),
        P("tp", None),
        P("tp", None),
        P("rep", "tp", None),
    )
    return jax.shard_map(
        body,
        mesh=mesh,
        in_specs=placed,
        out_specs=(
            P("rep", None, "tp"),
            P("rep", None, "tp"),
            P("rep", None, "tp"),
            P("rep", None),
            P("rep", "tp", None),
            P("tp", None),
            P("tp", None),
        ),
        check_vma=False,
    )
```

profile of v0, /device:TPU:0, one launch (start us, length us, event | category | flops | bytes accessed | tf_op | source)
XLA Modules:
  0.0 146.9 jit_solution(9005998716346742518)
XLA Ops:
  8.0 0.0 copy-start
  8.0 0.0 copy-start.19
  8.0 0.0 all-gather.2.cloned.1.call-start
  8.1 1.6 %fusion.25 = f32[128]{0:T(128)S(1)} fusion(bf16[1,128,3072]{2,1,0:T(8,128)(2,1)} %param.9), kind=kLoop, calls=%fused_computation.37 | loop fusion | flops 1179520 | bytes 786944 | tf_op jit(solution)/shard_map/reduce_sum | solution.py:102
  9.6 2.3 %fusion.22 = bf16[128,3072]{1,0:T(8,128)(2,1)} fusion(bf16[1,128,3072]{2,1,0:T(8,128)(2,1)} %param.9, f32[3072]{0:T(1024)} %bitcast.153, f32[128]{0:T(128)S(1)} %add_rsqrt_fusion), kind=kLoop, calls=%fused_computation.34 | loop fusion | flops 1572864 | bytes 1585664 | tf_op jit(solution)/shard_map/convert_element_type | solution.py:105
  11.9 0.0 all-gather.2.cloned.1.call-update
  11.9 0.0 all-reduce.2.cloned.1.call-start
  12.0 0.0 copy-done.19
  12.0 2.1 %convert_subtract_fusion = f32[64,3072]{1,0:T(8,128)} fusion(f32[64,3072]{1,0:T(8,128)} %param.15, bf16[1,64,3072]{2,1,0:T(8,128)(2,1)S(1)} %copy-done.19), kind=kLoop, calls=%fused_computation.65 | loop fusion | flops 393216 | bytes 1966080 | tf_op jit(solution)/shard_map/sub | solution.py:183
  14.1 0.0 all-reduce.2.cloned.1.call-update
  14.1 0.0 reduce-scatter.2.cloned.1.call-start
  14.2 8.7 %copy.38 = bf16[1024,3072]{1,0:T(8,128)(2,1)} copy(bf16[1024,3072]{0,1:T(8,128)(2,1)} %bitcast.138) | data formatting | bytes 12582912 | tf_op jit(solution)/shard_map/dot_general | solution.py:111
  22.9 0.1 iota_multiply_fusion
  23.0 0.5 fusion.56
  23.4 4.7 %copy.35 = bf16[512,3072]{1,0:T(8,128)(2,1)} copy(bf16[512,3072]{0,1:T(8,128)(2,1)} %bitcast.137) | data formatting | bytes 6291456 | tf_op jit(solution)/shard_map/dot_general | solution.py:115
  28.1 2.0 %copy.41 = bf16[1,256,1024]{1,2,0:T(8,128)(2,1)} copy(bf16[1,256,1024]{2,1,0:T(8,128)(2,1)} %param.14) | data formatting | bytes 1048576 | tf_op jit(solution)/shard_map/reshape;squeeze | solution.py:130
  30.2 11.8 %all-gather.2.cloned.1.call-done = bf16[256,3072]{1,0:T(8,128)(2,1)} async-done(((bf16[128,3072]{1,0:T(8,128)(2,1)}), bf16[256,3072]{1,0:T(8,128)(2,1)}) %all-gather.2.cloned.1.call-update) | async-done | bytes 1572880 | tf_op jit(solution)/shard_map/all_gather | solution.py:106
  42.0 5.3 %fusion.26 = f32[256,8,128]{0,2,1:T(8,128)S(1)} fusion(bf16[8,128,3072]{2,1,0:T(8,128)(2,1)} %bitcast.141, bf16[256,3072]{1,0:T(8,128)(2,1)} %all-gather.2.cloned.1.call-done), kind=kOutput, calls=%fused_computation.38 | convolution fusion | flops 1610612736 | bytes 8912896 | tf_op jit(solution)/shard_map/dot_general | solution.py:111
  47.3 0.0 copy-start.7
  47.3 0.0 copy-start.1
  47.3 1.1 slice_negate_fusion.1
  48.4 1.1 copy-done.1
  49.5 1.1 fusion.28
  50.5 0.0 copy-start.9
  50.5 0.9 slice_negate_fusion.3
  51.5 0.0 copy-done.9
  51.5 0.0 copy-done
  51.5 1.7 %fusion.30 = bf16[256,512]{1,0:T(8,128)(2,1)} fusion(bf16[256,3072]{1,0:T(8,128)(2,1)S(1)} %copy-done.1, bf16[1,3072,512]{2,1,0:T(8,128)(2,1)S(1)} %copy-done), kind=kOutput, calls=%fused_computation.44 | convolution fusion | flops 805437440 | bytes 4980736 | tf_op jit(solution)/shard_map/dot_general | solution.py:120
  53.2 1.7 %reshape.115 = bf16[256,4,128]{2,1,0:T(4,128)(2,1)} reshape(bf16[256,512]{1,0:T(8,128)(2,1)} %fusion.30) | data formatting | bytes 524288 | tf_op jit(solution)/shard_map/reshape | solution.py:122
  55.0 2.7 %fusion.35 = bf16[256,8,128]{0,2,1:T(8,128)(2,1)} fusion(f32[256,8,64]{0,2,1:T(8,128)} %get-tuple-element.40, f32[256,8,64]{0,2,1:T(8,128)} %get-tuple-element.39, f32[256,8,128]{0,2,1:T(8,128)} %copy-done.7, f32[256,128]{0,1:T(8,128)S(1)} %get-tuple-element.46, f32[256,128]{0,1:T(8,128)S(1)} %get-tuple-element.45), kind=kLoop, calls=%fused_computation.48 | loop fusion | flops 1310720 | bytes 2883584 | tf_op jit(solution)/shard_map/convert_element_type | solution.py:114
  57.7 0.0 copy-done.14
  57.7 0.8 fusion.50
  58.5 0.0 copy-done.11
  58.5 1.7 %fusion.51 = f32[4,256,256,2]{2,1,3,0:T(8,128)} fusion(bf16[256,4,2,128]{0,3,2,1:T(8,128)(2,1)S(1)} %bitcast.146, bf16[256,4,128,1]{2,1,0,3:T(4,128)(2,1)S(1)} %bitcast.149), kind=kOutput, calls=%fused_computation.78 | convolution fusion | flops 134217728 | bytes 2883584 | tf_op jit(solution)/shard_map/while/body/eval_jaxpr/qgrd,kgd->grqk/dot_general | solution.py:60
  60.2 3.3 %fusion.65 = (f32[4,2,256]{2,1,0:T(2,128)S(1)}, f32[4,2,256,256]{2,3,1,0:T(8,128)}) fusion(pred[256,256]{0,1:T(8,128)(4,1)S(1)} %iota_compare_fusion, bf16[256,4,128,1]{0,2,3,1:T(8,128)(2,1)} %fusion.50, bf16[256,4,2,128]{0,3,2,1:T(8,128)(2,1)} %bitcast.150), kind=kOutput, calls=%fused_computation.98 | convolution fusion | flops 136315136 | bytes 2957312 | tf_op jit(solution)/shard_map/while/body/eval_jaxpr/sub | solution.py:54
  63.5 5.4 %broadcast_multiply_fusion = (f32[256,4,128]{0,2,1:T(8,128)}, f32[256,4,128]{0,2,1:T(8,128)}) fusion(f32[256,128]{0,1:T(8,128)S(1)} %get-tuple-element.46, bf16[256,4,2,128]{0,3,2,1:T(8,128)(2,1)} %bitcast.151, f32[4,256,256,2]{2,1,3,0:T(8,128)} %fusion.51, f32[4,2,256,256]{2,3,1,0:T(8,128)} %get-tuple-element.48, f32[4,2,256]{2,1,0:T(2,128)S(1)} %get-tuple-element.47), kind=kOutput, calls=%fused_computation.81 | convolution fusion | flops 138021120 | bytes 5906432 | tf_op jit(solution)/shard_map/while/body/eval_jaxpr/grqk,qgrd->kgd/dot_general | solution.py:72
  68.8 5.3 %fusion.44 = f32[4,128,2,256]{3,1,2,0:T(8,128)} fusion(bf16[256,4,128,1]{0,2,3,1:T(8,128)(2,1)} %fusion.50, f32[4,256,256,2]{2,1,3,0:T(8,128)} %fusion.51, f32[4,2,256,256]{2,3,1,0:T(8,128)} %get-tuple-element.48, f32[4,2,256]{2,1,0:T(2,128)S(1)} %get-tuple-element.47), kind=kOutput, calls=%fused_computation.62 | convolution fusion | flops 137890048 | bytes 5513216 | tf_op jit(solution)/shard_map/while/body/eval_jaxpr/grqk,kgd->qgrd/dot_general | solution.py:69
  74.2 2.3 %fusion.33 = bf16[4,256,128]{1,2,0:T(8,128)(2,1)S(1)} fusion(bf16[256,4,2,128]{0,3,2,1:T(8,128)(2,1)} %bitcast.145, f32[4,2,256,256]{2,3,1,0:T(8,128)} %get-tuple-element.48, f32[4,2,256]{2,1,0:T(2,128)S(1)} %get-tuple-element.47), kind=kOutput, calls=%fused_computation.45 | convolution fusion | flops 135397376 | bytes 2891776 | tf_op jit(solution)/shard_map/while/body/eval_jaxpr/grqk,qgrd->kgd/dot_general | solution.py:57
  76.5 0.0 copy-start.12
  76.5 0.0 slice-start.1
  76.6 0.1 bitcast_multiply_fusion.3
  76.7 0.1 fusion.63
  76.7 1.1 fusion.39
  77.9 0.0 slice-done
  77.9 1.1 slice-done.1
  79.0 1.8 %fusion.2 = f32[256,3072]{1,0:T(8,128)S(1)} fusion(bf16[256,1024]{0,1:T(8,128)(2,1)S(1)} %bitcast.152, bf16[1,3072,1024]{2,1,0:T(8,128)(2,1)S(1)} %bitcast.140), kind=kOutput, calls=%fused_computation.2 | convolution fusion | flops 1610612736 | bytes 9961472 | tf_op jit(solution)/shard_map/dot_general | solution.py:161
  80.8 0.0 copy-done.18
  80.8 0.1 fusion.49
  80.9 0.1 copy-done.3
  81.0 1.1 convolution_add_fusion.1
  82.1 2.2 %fusion.6 = bf16[256,3072]{1,0:T(8,128)(2,1)} fusion(f32[256,3072]{1,0:T(8,128)S(1)} %convolution_add_fusion.1, bf16[256,512]{0,1:T(8,128)(2,1)S(1)} %bitcast.147, bf16[1,3072,512]{2,1,0:T(8,128)(2,1)S(1)} %copy-done), kind=kOutput, calls=%fused_computation.11 | convolution fusion | flops 806879232 | bytes 8126464 | tf_op jit(solution)/shard_map/dot_general | solution.py:168
  84.3 0.0 reduce-scatter.2.cloned.1.call-update
  84.3 27.0 %all-reduce.2.cloned.1.call-done = f32[64,3072]{1,0:T(8,128)} async-done(((f32[64,3072]{1,0:T(8,128)}), f32[64,3072]{1,0:T(8,128)}) %all-reduce.2.cloned.1.call-update) | async-done | bytes 786448 | tf_op jit(solution)/shard_map/psum | solution.py:185
  111.3 3.1 %multiply_subtract_fusion = (f32[64,3072]{1,0:T(8,128)}, f32[64,3072]{1,0:T(8,128)}) fusion(f32[64,3072]{1,0:T(8,128)} %param.15, f32[64,3072]{1,0:T(8,128)} %all-reduce.2.cloned.1.call-done, f32[64,3072]{1,0:T(8,128)} %param.16), kind=kLoop, calls=%fused_computation.66 | loop fusion | flops 1376256 | bytes 3932160 | tf_op jit(solution)/shard_map/sub | solution.py:187
  114.5 0.0 copy-done.6
  114.5 0.2 fusion.37
  114.7 1.2 copy-done.2
  115.9 0.0 copy-done.13
  115.9 2.9 %fusion.5 = bf16[1,3072,512]{2,1,0:T(8,128)(2,1)} fusion(bf16[256,3072]{1,0:T(8,128)(2,1)S(1)} %copy-done.2, bf16[256,512]{0,1:T(8,128)(2,1)S(1)} %bitcast.148), kind=kOutput, calls=%fused_computation.8 | convolution fusion | flops 806879232 | bytes 4980736 | tf_op jit(solution)/shard_map/dot_general | solution.py:157
  118.8 2.7 %fusion.4 = bf16[1,3072,512]{2,1,0:T(8,128)(2,1)} fusion(bf16[256,3072]{1,0:T(8,128)(2,1)S(1)} %copy-done.2, bf16[256,512]{0,1:T(8,128)(2,1)S(1)} %bitcast.144), kind=kOutput, calls=%fused_computation.7 | convolution fusion | flops 806879232 | bytes 4980736 | tf_op jit(solution)/shard_map/dot_general | solution.py:154
  121.5 4.6 %convert_bitcast_fusion = bf16[1,3072,1024]{2,1,0:T(8,128)(2,1)} fusion(bf16[256,3072]{1,0:T(8,128)(2,1)S(1)} %copy-done.2, bf16[256,1024]{0,1:T(8,128)(2,1)S(1)} %fusion.37), kind=kOutput, calls=%fused_computation.4 | convolution fusion | flops 1613758464 | bytes 8388608 | tf_op jit(solution)/shard_map/dot_general | solution.py:151
  126.1 1.9 %fusion.24 = (f32[128]{0:T(128)S(1)}, f32[3072]{0:T(1024)S(1)}) fusion(bf16[128,3072]{1,0:T(8,128)(2,1)} %reduce-scatter.2.cloned.1.call-done, bf16[1,128,3072]{2,1,0:T(8,128)(2,1)} %param.9, f32[3072]{0:T(1024)S(1)} %bitcast.154, f32[128]{0:T(128)S(1)} %add_rsqrt_fusion), kind=kLoop, calls=%fused_computation.36 | loop fusion | flops 3142528 | bytes 1598464 | tf_op jit(solution)/shard_map/reduce_sum | solution.py:180
  128.0 8.8 %psum.14 = f32[1,3072]{1,0:T(1,128)} all-reduce(f32[1,3072]{1,0:T(1,128)S(1)} %bitcast.156), channel_id=1, replica_groups=mesh['rep'=16,'tp'=2] {'tp'}, use_global_device_ids=true, to_apply=%region_6.7 | all-reduce | flops 3072 | bytes 24576 | tf_op jit(solution)/shard_map/psum | solution.py:174
  136.8 2.7 %fusion.46 = bf16[1,128,3072]{2,1,0:T(8,128)(2,1)} fusion(bf16[128,3072]{1,0:T(8,128)(2,1)} %reduce-scatter.2.cloned.1.call-done, bf16[1,128,3072]{2,1,0:T(8,128)(2,1)} %param.9, f32[128]{0:T(128)S(1)} %broadcast_multiply_fusion.1, f32[3072]{0:T(1024)S(1)} %bitcast.155, f32[128]{0:T(128)S(1)} %add_rsqrt_fusion), kind=kLoop, calls=%fused_computation.64 | loop fusion | flops 3145728 | bytes 2372608 | tf_op jit(solution)/shard_map/broadcast_in_dim | solution.py:193
  (33 shorter events, 0.1 us)
Async XLA Ops:
  8.0 43.5 %copy-start = (bf16[1,3072,512]{2,1,0:T(8,128)(2,1)S(1)}, bf16[1,3072,512]{2,1,0:T(8,128)(2,1)}, u32[]{:S(2)}) copy-start(bf16[1,3072,512]{2,1,0:T(8,128)(2,1)} %param.13) | copy-start | bytes 9437188
  8.0 4.0 %copy-start.19 = (bf16[1,64,3072]{2,1,0:T(8,128)(2,1)S(1)}, bf16[1,64,3072]{2,1,0:T(8,128)(2,1)}, u32[]{:S(2)}) copy-start(bf16[1,64,3072]{2,1,0:T(8,128)(2,1)} %param.17) | copy-start | bytes 1179652
  8.0 34.0 %all-gather.2.cloned.1.call-start = ((), (), s32[]{:S(2)}) async-start(), calls=%async_computation.1 | async-start | bytes 2359296 | tf_op jit(solution)/shard_map/all_gather | solution.py:106
  11.9 99.4 %all-reduce.2.cloned.1.call-start = ((), (), s32[]{:S(2)}) async-start(), calls=%async_computation.3 | async-start | bytes 1572864 | tf_op jit(solution)/shard_map/psum | solution.py:185
  14.1 112.0 %reduce-scatter.2.cloned.1.call-start = ((), (), s32[]{:S(2)}) async-start(), calls=%async_computation.2 | async-start | bytes 2359296 | tf_op jit(solution)/shard_map/reduce_scatter | solution.py:165
  42.0 6.4 %copy-start.8 = (bf16[512,3072]{1,0:T(8,128)(2,1)S(1)}, bf16[512,3072]{1,0:T(8,128)(2,1)}, u32[]{:S(2)}) copy-start(bf16[512,3072]{1,0:T(8,128)(2,1)} %copy.35) | copy-start | bytes 9437188
  47.3 3.2 %copy-start.7 = (f32[256,8,128]{0,2,1:T(8,128)}, f32[256,8,128]{0,2,1:T(8,128)S(1)}, u32[]{:S(2)}) copy-start(f32[256,8,128]{0,2,1:T(8,128)S(1)} %fusion.26) | copy-start | bytes 3145732
  47.3 2.2 %copy-start.1 = (bf16[256,3072]{1,0:T(8,128)(2,1)S(1)}, bf16[256,3072]{1,0:T(8,128)(2,1)}, u32[]{:S(2)}) copy-start(bf16[256,3072]{1,0:T(8,128)(2,1)} %all-gather.2.cloned.1.call-done) | copy-start | bytes 4718596
  50.5 1.0 copy-start.9
  55.0 2.7 %copy-start.10 = (f32[256,4,128]{0,2,1:T(8,128)S(1)}, f32[256,4,128]{0,2,1:T(8,128)}, u32[]{:S(2)}) copy-start(f32[256,4,128]{0,2,1:T(8,128)} %copy-done.9) | copy-start | bytes 1572868
  55.0 2.7 %copy-start.14 = (f32[256,4,64]{0,2,1:T(8,128)S(1)}, f32[256,4,64]{0,2,1:T(8,128)}, u32[]{:S(2)}) copy-start(f32[256,4,64]{0,2,1:T(8,128)} %get-tuple-element.43) | copy-start | bytes 786436
  55.0 2.7 %copy-start.15 = (f32[256,4,64]{0,2,1:T(8,128)S(1)}, f32[256,4,64]{0,2,1:T(8,128)}, u32[]{:S(2)}) copy-start(f32[256,4,64]{0,2,1:T(8,128)} %get-tuple-element.44) | copy-start | bytes 786436
  55.0 3.5 %copy-start.11 = (bf16[1,256,1024]{1,2,0:T(8,128)(2,1)S(1)}, bf16[1,256,1024]{1,2,0:T(8,128)(2,1)}, u32[]{:S(2)}) copy-start(bf16[1,256,1024]{1,2,0:T(8,128)(2,1)} %copy.41) | copy-start | bytes 1572868
  55.0 3.5 %copy-start.16 = (bf16[256,4,128]{2,1,0:T(4,128)(2,1)S(1)}, bf16[256,4,128]{2,1,0:T(4,128)(2,1)}, u32[]{:S(2)}) copy-start(bf16[256,4,128]{2,1,0:T(4,128)(2,1)} %reshape.115) | copy-start | bytes 786436
  74.2 2.3 %copy-start.17 = (f32[256,4,128]{0,2,1:T(8,128)S(1)}, f32[256,4,128]{0,2,1:T(8,128)}, u32[]{:S(2)}) copy-start(f32[256,4,128]{0,2,1:T(8,128)} %get-tuple-element.49) | copy-start | bytes 1572868
  74.2 2.4 %copy-start.4 = (f32[4,128,2,256]{3,1,2,0:T(8,128)S(1)}, f32[4,128,2,256]{3,1,2,0:T(8,128)}, u32[]{:S(2)}) copy-start(f32[4,128,2,256]{3,1,2,0:T(8,128)} %fusion.44) | copy-start | bytes 3145732
  74.2 3.7 %slice-start = ((s8[6291456]{0:T(1024)(128)(4,1)}), s8[4194304]{0:T(1024)(128)(4,1)S(1)}, s32[]{:S(2)}) async-start(s8[6291456]{0:T(1024)(128)(4,1)} %bitcast.139), calls=%async_computation.4 | async-start | bytes 8388608
  76.5 5.6 %copy-start.12 = (bf16[4,256,128]{1,2,0:T(8,128)(2,1)}, bf16[4,256,128]{1,2,0:T(8,128)(2,1)S(1)}, u32[]{:S(2)}) copy-start(bf16[4,256,128]{1,2,0:T(8,128)(2,1)S(1)} %fusion.33) | copy-start | bytes 786436
  76.5 2.5 %slice-start.1 = ((s8[6291456]{0:T(1024)(128)(4,1)}), s8[2097152]{0:T(1024)(128)(4,1)S(1)}, s32[]{:S(2)}) async-start(s8[6291456]{0:T(1024)(128)(4,1)} %bitcast.139), calls=%async_computation.5 | async-start | bytes 4194304
  79.0 1.9 %copy-start.18 = (f32[256,4,128]{0,2,1:T(8,128)S(1)}, f32[256,4,128]{0,2,1:T(8,128)}, u32[]{:S(2)}) copy-start(f32[256,4,128]{0,2,1:T(8,128)} %get-tuple-element.50) | copy-start | bytes 1572868
  79.0 2.1 %copy-start.3 = (bf16[1,3072,512]{2,1,0:T(8,128)(2,1)S(1)}, bf16[1,3072,512]{2,1,0:T(8,128)(2,1)}, u32[]{:S(2)}) copy-start(bf16[1,3072,512]{2,1,0:T(8,128)(2,1)} %param.12) | copy-start | bytes 9437188
  111.3 3.1 %copy-start.5 = (f32[4,128,2,256]{3,1,2,0:T(8,128)S(1)}, f32[4,128,2,256]{3,1,2,0:T(8,128)}, u32[]{:S(2)}) copy-start(f32[4,128,2,256]{3,1,2,0:T(8,128)} %fusion.44) | copy-start | bytes 3145732
  111.3 3.1 %copy-start.6 = (f32[256,8,128]{0,2,1:T(8,128)S(1)}, f32[256,8,128]{0,2,1:T(8,128)}, u32[]{:S(2)}) copy-start(f32[256,8,128]{0,2,1:T(8,128)} %get-tuple-element.36) | copy-start | bytes 3145732
  114.5 1.4 copy-start.2
  114.5 1.4 copy-start.13
  121.5 4.6 %copy-start.20 = (f32[1,3072]{1,0:T(1,128)S(1)}, f32[1,3072]{1,0:T(1,128)}, u32[]{:S(2)}) copy-start(f32[1,3072]{1,0:T(1,128)} %param.10) | copy-start | bytes 36868
Sparse Core Ops, SparseCore 0:
  12.1 29.9 all-gather.1
  84.5 26.1 reduce-scatter.1
Sparse Core Ops, SparseCore 1:
  16.4 94.9 all-reduce.1
where the time goes:
time: 148 us; the launch traced here: 147 us
  matrix products  41.3 us (28%)
  waiting for transfers between devices  38.9 us (26%)
  other arithmetic  21.3 us (14%)
  local copies, waits for them, and re-layouts  20.8 us (14%)
  between operations  15.7 us (11%)
  blocking collectives  8.76 us (6%)
    psum x1, waiting for transfers between devices, body(): mean_delta = lax.psum(delta, 'rep') / replicas  27 us
    all_gather x1, waiting for transfers between devices, body(): normalized = lax.all_gather(normalized_local, 'tp', axis=0, tiled=True)  11.8 us
    psum x1, blocking collectives, body(): lax.psum(jnp.sum(summed_rows * normalized_input, axis=0), 'tp')  8.76 us
    dot_general x1, local copies, waits for them, and re-layouts, body(): jnp.dot(normalized, weight_q, preferred_element_type=jnp.float32)  8.68 us
    dot_general x1, matrix products, one_block(): jnp.einsum('grqk,qgrd->kgd', score_low, query_block, preferred_element_ty...  5.36 us
    dot_general x1, matrix products, one_block(): jnp.einsum('grqk,kgd->qgrd', score_low, rotated_keys, preferred_element_t...  5.3 us
    dot_general x1, matrix products, body(): jnp.dot(normalized, weight_q, preferred_element_type=jnp.float32)  5.26 us
    dot_general x1, local copies, waits for them, and re-layouts, body(): jnp.dot(normalized, weight_k, preferred_element_type=jnp.float32)  4.69 us
  transfers between devices with their start and end apart: 3, of which 2 were waited for; matrix products, arithmetic and copies ran while one was open for 49% of the time, Pallas kernels for 0%

commit v1 on v0

--- a/solution.py
+++ b/solution.py
@@ -103,7 +103,14 @@
     )
     normalized_input = widened_rows * inverse_norm
     normalized_local = (normalized_input * norm_gains[None, :]).astype(jnp.bfloat16)
-    normalized = lax.all_gather(normalized_local, "tp", axis=0, tiled=True)
+    list_strings = lambda field: jnp.roll(
+        jnp.concatenate(
+            [field, lax.ppermute(field, perm=[(0, 1), (1, 0)], axis_name="tp")], axis=0
+        ),
+        lax.axis_index("tp") * field.shape[0],
+        axis=0,
+    )
+    normalized = list_strings(normalized_local)
     sequence_length = normalized.shape[0]
     heads_q = weight_q.shape[1] // HEAD_SIZE
     heads_kv = weight_k.shape[1] // HEAD_SIZE

time: 148 us -> 145 us (0.980)
  waiting for transfers between devices: 38.9 us -> 32.6 us
  starting transfers between devices: 0.12 us -> 3.08 us
  other arithmetic: 21.3 us -> 23.4 us
    all_gather x1 -> x0, waiting for transfers between devices: 11.8 us -> none  [body(): normalized = lax.all_gather(normalized_local, 'tp', axis=0, tiled=True)]
    psum x1, waiting for transfers between devices: 27 us -> 31.6 us  [body(): mean_delta = lax.psum(delta, 'rep') / replicas]
    concatenate x0 -> x1, other arithmetic: none -> 3.09 us  [body(): jnp.roll(jnp.concatenate([field, lax.ppermute(field, perm=[(0, 1), (1, 0)...]
    ppermute x0 -> x1, starting transfers between devices: none -> 3 us  [body(): lax.ppermute(field, perm=[(0, 1), (1, 0)], axis_name='tp')]
    unnamed x46 -> x48, local copies, waits for them, and re-layouts: 3.6 us -> 2.51 us
  transfers between devices with their start and end apart: 3 -> 3, of which waited for: 2 -> 2; matrix products, arithmetic and copies ran while one was open for 49% -> 51% of each run, Pallas kernels for 0% -> 0%
where the time goes in v1:
time: 145 us; the launch traced here: 144 us
  matrix products  41.3 us (28%)
  waiting for transfers between devices  32.6 us (22%)
  other arithmetic  23.4 us (16%)
  local copies, waits for them, and re-layouts  19.5 us (13%)
  between operations  15.7 us (11%)
  blocking collectives  8.59 us (6%)
  starting transfers between devices  3.08 us (2%)
    psum x1, waiting for transfers between devices, body(): mean_delta = lax.psum(delta, 'rep') / replicas  31.6 us
    dot_general x1, local copies, waits for them, and re-layouts, body(): jnp.dot(normalized, weight_q, preferred_element_type=jnp.float32)  8.62 us
    psum x1, blocking collectives, body(): lax.psum(jnp.sum(summed_rows * normalized_input, axis=0), 'tp')  8.59 us
    dot_general x1, matrix products, one_block(): jnp.einsum('grqk,qgrd->kgd', score_low, query_block, preferred_element_ty...  5.38 us
    dot_general x1, matrix products, one_block(): jnp.einsum('grqk,kgd->qgrd', score_low, rotated_keys, preferred_element_t...  5.29 us
    dot_general x1, matrix products, body(): jnp.dot(normalized, weight_q, preferred_element_type=jnp.float32)  5.28 us
    dot_general x1, local copies, waits for them, and re-layouts, body(): jnp.dot(normalized, weight_k, preferred_element_type=jnp.float32)  4.63 us
    dot_general x1, matrix products, body(): lax.dot_general(normalized, dquery, contract, preferred_element_type=jnp....  4.57 us
  transfers between devices with their start and end apart: 3, of which 2 were waited for; matrix products, arithmetic and copies ran while one was open for 51% of the time, Pallas kernels for 0%

profile of v1, /device:TPU:0, one launch (start us, length us, event | category | flops | bytes accessed | tf_op | source)
XLA Modules:
  0.0 144.3 jit_solution(2043605847415790632)
XLA Ops:
  8.0 0.0 copy-start
  8.0 0.0 copy-start.20
  8.0 0.0 all-reduce.2.cloned.1.call-start
  8.1 0.0 copy-start.9
  8.1 1.5 %fusion.25 = f32[128]{0:T(128)S(1)} fusion(bf16[1,128,3072]{2,1,0:T(8,128)(2,1)} %param.9), kind=kLoop, calls=%fused_computation.41 | loop fusion | flops 1179520 | bytes 786944 | tf_op jit(solution)/shard_map/reduce_sum | solution.py:102
  9.6 2.3 %fusion.22 = bf16[128,3072]{1,0:T(8,128)(2,1)} fusion(bf16[1,128,3072]{2,1,0:T(8,128)(2,1)} %param.9, f32[3072]{0:T(1024)} %bitcast.153, f32[128]{0:T(128)S(1)} %add_rsqrt_fusion), kind=kLoop, calls=%fused_computation.38 | loop fusion | flops 1572864 | bytes 1585664 | tf_op jit(solution)/shard_map/convert_element_type | solution.py:105
  11.9 3.0 %collective-permute-start = (bf16[128,3072]{1,0:T(8,128)(2,1)}, bf16[128,3072]{1,0:T(8,128)(2,1)}, u32[]{:S(2)}, u32[]{:S(2)}) collective-permute-start(bf16[128,3072]{1,0:T(8,128)(2,1)} %fusion.22), channel_id=1, source_target_pairs={{0,1},{1,0},{2,3},{3,2},{4,5},{5,4},{6,7},{7,6},{8,9},{9,8},{10,11... | collective-permute-start | bytes 2359304 | tf_op jit(solution)/shard_map/ppermute | solution.py:108
  14.9 0.0 copy-done.20
  14.9 0.0 copy-done.9
  14.9 0.9 convert_subtract_fusion
  15.8 0.0 all-reduce.2.cloned.1.call-update
  15.9 0.0 reduce-scatter.2.cloned.1.call-start
  15.9 8.6 %copy.38 = bf16[1024,3072]{1,0:T(8,128)(2,1)} copy(bf16[1024,3072]{0,1:T(8,128)(2,1)} %bitcast.138) | data formatting | bytes 12582912 | tf_op jit(solution)/shard_map/dot_general | solution.py:118
  24.6 4.6 %copy.35 = bf16[512,3072]{1,0:T(8,128)(2,1)} copy(bf16[512,3072]{0,1:T(8,128)(2,1)} %bitcast.137) | data formatting | bytes 6291456 | tf_op jit(solution)/shard_map/dot_general | solution.py:122
  29.2 2.0 %copy.41 = bf16[1,256,1024]{1,2,0:T(8,128)(2,1)} copy(bf16[1,256,1024]{2,1,0:T(8,128)(2,1)} %param.14) | data formatting | bytes 1048576 | tf_op jit(solution)/shard_map/reshape;squeeze | solution.py:137
  31.3 0.1 iota_multiply_fusion
  31.4 0.5 fusion.59
  31.8 0.9 collective-permute-done
  32.7 3.1 %fusion.28 = bf16[256,3072]{1,0:T(8,128)(2,1)S(1)} fusion(s32[]{:T(128)S(6)} %select_n.22, bf16[128,3072]{1,0:T(8,128)(2,1)} %fusion.22, bf16[128,3072]{1,0:T(8,128)(2,1)} %collective-permute-done), kind=kLoop, calls=%fused_computation.44 | loop fusion | flops 6291456 | bytes 3145732 | tf_op jit(solution)/shard_map/jit(_roll_dynamic)/concatenate | solution.py:106
  35.8 0.0 copy-start.1
  35.9 0.0 copy-start.8
  35.9 5.3 %fusion.29 = f32[256,8,128]{0,2,1:T(8,128)S(1)} fusion(bf16[8,128,3072]{2,1,0:T(8,128)(2,1)} %bitcast.141, bf16[256,3072]{1,0:T(8,128)(2,1)S(1)} %fusion.28), kind=kOutput, calls=%fused_computation.45 | convolution fusion | flops 1610612736 | bytes 8912896 | tf_op jit(solution)/shard_map/dot_general | solution.py:118
  41.1 0.0 copy-start.7
  41.2 1.1 slice_negate_fusion.1
  42.3 1.0 fusion.31
  43.3 0.0 copy-start.10
  43.3 1.0 slice_negate_fusion.3
  44.3 0.0 copy-done.10
  44.3 1.7 %fusion.33 = bf16[256,512]{1,0:T(8,128)(2,1)} fusion(bf16[256,3072]{1,0:T(8,128)(2,1)S(1)} %fusion.28, bf16[1,3072,512]{2,1,0:T(8,128)(2,1)S(1)} %copy-done), kind=kOutput, calls=%fused_computation.51 | convolution fusion | flops 805437440 | bytes 4980736 | tf_op jit(solution)/shard_map/dot_general | solution.py:127
  46.0 1.7 %reshape.115 = bf16[256,4,128]{2,1,0:T(4,128)(2,1)} reshape(bf16[256,512]{1,0:T(8,128)(2,1)} %fusion.33) | data formatting | bytes 524288 | tf_op jit(solution)/shard_map/reshape | solution.py:129
  47.8 0.0 copy-start.17
  47.8 2.7 %fusion.38 = bf16[256,8,128]{0,2,1:T(8,128)(2,1)} fusion(f32[256,8,64]{0,2,1:T(8,128)} %get-tuple-element.40, f32[256,8,64]{0,2,1:T(8,128)} %get-tuple-element.39, f32[256,8,128]{0,2,1:T(8,128)} %copy-done.7, f32[256,128]{0,1:T(8,128)S(1)} %get-tuple-element.46, f32[256,128]{0,1:T(8,128)S(1)} %get-tuple-element.45), kind=kLoop, calls=%fused_computation.55 | loop fusion | flops 1310720 | bytes 2883584 | tf_op jit(solution)/shard_map/convert_element_type | solution.py:121
  50.5 0.8 fusion.53
  51.3 1.7 %fusion.54 = f32[4,256,256,2]{2,1,3,0:T(8,128)} fusion(bf16[256,4,2,128]{0,3,2,1:T(8,128)(2,1)S(1)} %bitcast.146, bf16[256,4,128,1]{2,1,0,3:T(4,128)(2,1)S(1)} %bitcast.149), kind=kOutput, calls=%fused_computation.85 | convolution fusion | flops 134217728 | bytes 2883584 | tf_op jit(solution)/shard_map/while/body/eval_jaxpr/qgrd,kgd->grqk/dot_general | solution.py:60
  53.1 3.3 %fusion.68 = (f32[4,2,256]{2,1,0:T(2,128)S(1)}, f32[4,2,256,256]{2,3,1,0:T(8,128)}) fusion(pred[256,256]{0,1:T(8,128)(4,1)S(1)} %iota_compare_fusion, bf16[256,4,128,1]{0,2,3,1:T(8,128)(2,1)} %fusion.53, bf16[256,4,2,128]{0,3,2,1:T(8,128)(2,1)} %bitcast.150), kind=kOutput, calls=%fused_computation.105 | convolution fusion | flops 136315136 | bytes 2957312 | tf_op jit(solution)/shard_map/while/body/eval_jaxpr/sub | solution.py:54
  56.3 5.4 %broadcast_multiply_fusion = (f32[256,4,128]{0,2,1:T(8,128)}, f32[256,4,128]{0,2,1:T(8,128)}) fusion(f32[256,128]{0,1:T(8,128)S(1)} %get-tuple-element.46, bf16[256,4,2,128]{0,3,2,1:T(8,128)(2,1)} %bitcast.151, f32[4,256,256,2]{2,1,3,0:T(8,128)} %fusion.54, f32[4,2,256,256]{2,3,1,0:T(8,128)} %get-tuple-element.48, f32[4,2,256]{2,1,0:T(2,128)S(1)} %get-tuple-element.47), kind=kOutput, calls=%fused_computation.88 | convolution fusion | flops 138021120 | bytes 5906432 | tf_op jit(solution)/shard_map/while/body/eval_jaxpr/grqk,qgrd->kgd/dot_general | solution.py:72
  61.7 5.3 %fusion.47 = f32[4,128,2,256]{3,1,2,0:T(8,128)} fusion(bf16[256,4,128,1]{0,2,3,1:T(8,128)(2,1)} %fusion.53, f32[4,256,256,2]{2,1,3,0:T(8,128)} %fusion.54, f32[4,2,256,256]{2,3,1,0:T(8,128)} %get-tuple-element.48, f32[4,2,256]{2,1,0:T(2,128)S(1)} %get-tuple-element.47), kind=kOutput, calls=%fused_computation.69 | convolution fusion | flops 137890048 | bytes 5513216 | tf_op jit(solution)/shard_map/while/body/eval_jaxpr/grqk,kgd->qgrd/dot_general | solution.py:69
  67.0 2.3 %fusion.36 = bf16[4,256,128]{1,2,0:T(8,128)(2,1)S(1)} fusion(bf16[256,4,2,128]{0,3,2,1:T(8,128)(2,1)} %bitcast.145, f32[4,2,256,256]{2,3,1,0:T(8,128)} %get-tuple-element.48, f32[4,2,256]{2,1,0:T(2,128)S(1)} %get-tuple-element.47), kind=kOutput, calls=%fused_computation.52 | convolution fusion | flops 135397376 | bytes 2891776 | tf_op jit(solution)/shard_map/while/body/eval_jaxpr/grqk,qgrd->kgd/dot_general | solution.py:57
  69.3 0.0 copy-start.13
  69.4 0.0 copy-done.18
  69.4 0.0 slice-start.1
  69.4 0.0 copy-done.4
  69.4 0.1 bitcast_multiply_fusion.3
  69.5 0.1 fusion.66
  69.6 1.1 fusion.42
  70.7 1.1 slice-done.1
  71.8 1.8 %fusion.2 = f32[256,3072]{1,0:T(8,128)S(1)} fusion(bf16[256,1024]{0,1:T(8,128)(2,1)S(1)} %bitcast.152, bf16[1,3072,1024]{2,1,0:T(8,128)(2,1)S(1)} %bitcast.140), kind=kOutput, calls=%fused_computation.2 | convolution fusion | flops 1610612736 | bytes 9961472 | tf_op jit(solution)/shard_map/dot_general | solution.py:168
  73.7 0.1 fusion.52
  73.8 0.1 copy-done.3
  73.9 1.3 convolution_add_fusion.1
  75.2 0.0 copy-done.13
  75.2 2.2 %fusion.6 = bf16[256,3072]{1,0:T(8,128)(2,1)} fusion(f32[256,3072]{1,0:T(8,128)S(1)} %convolution_add_fusion.1, bf16[256,512]{0,1:T(8,128)(2,1)S(1)} %bitcast.147, bf16[1,3072,512]{2,1,0:T(8,128)(2,1)S(1)} %copy-done), kind=kOutput, calls=%fused_computation.11 | convolution fusion | flops 806879232 | bytes 8126464 | tf_op jit(solution)/shard_map/dot_general | solution.py:175
  77.4 0.0 reduce-scatter.2.cloned.1.call-update
  77.4 31.6 %all-reduce.2.cloned.1.call-done = f32[64,3072]{1,0:T(8,128)} async-done(((f32[64,3072]{1,0:T(8,128)}), f32[64,3072]{1,0:T(8,128)}) %all-reduce.2.cloned.1.call-update) | async-done | bytes 786448 | tf_op jit(solution)/shard_map/psum | solution.py:192
  109.1 3.1 %multiply_subtract_fusion = (f32[64,3072]{1,0:T(8,128)}, f32[64,3072]{1,0:T(8,128)}) fusion(f32[64,3072]{1,0:T(8,128)} %param.15, f32[64,3072]{1,0:T(8,128)} %all-reduce.2.cloned.1.call-done, f32[64,3072]{1,0:T(8,128)} %param.16), kind=kLoop, calls=%fused_computation.73 | loop fusion | flops 1376256 | bytes 3932160 | tf_op jit(solution)/shard_map/sub | solution.py:194
  112.2 0.2 fusion.40
  112.4 1.2 copy-done.2
  113.6 0.0 copy-done.14
  113.6 2.7 %fusion.5 = bf16[1,3072,512]{2,1,0:T(8,128)(2,1)} fusion(bf16[256,3072]{1,0:T(8,128)(2,1)S(1)} %copy-done.2, bf16[256,512]{0,1:T(8,128)(2,1)S(1)} %bitcast.148), kind=kOutput, calls=%fused_computation.8 | convolution fusion | flops 806879232 | bytes 4980736 | tf_op jit(solution)/shard_map/dot_general | solution.py:164
  116.3 2.7 %fusion.4 = bf16[1,3072,512]{2,1,0:T(8,128)(2,1)} fusion(bf16[256,3072]{1,0:T(8,128)(2,1)S(1)} %copy-done.2, bf16[256,512]{0,1:T(8,128)(2,1)S(1)} %bitcast.144), kind=kOutput, calls=%fused_computation.7 | convolution fusion | flops 806879232 | bytes 4980736 | tf_op jit(solution)/shard_map/dot_general | solution.py:161
  119.0 4.6 %convert_bitcast_fusion = bf16[1,3072,1024]{2,1,0:T(8,128)(2,1)} fusion(bf16[256,3072]{1,0:T(8,128)(2,1)S(1)} %copy-done.2, bf16[256,1024]{0,1:T(8,128)(2,1)S(1)} %fusion.40), kind=kOutput, calls=%fused_computation.4 | convolution fusion | flops 1613758464 | bytes 8388608 | tf_op jit(solution)/shard_map/dot_general | solution.py:158
  123.6 1.9 %fusion.24 = (f32[128]{0:T(128)S(1)}, f32[3072]{0:T(1024)S(1)}) fusion(bf16[128,3072]{1,0:T(8,128)(2,1)} %reduce-scatter.2.cloned.1.call-done, bf16[1,128,3072]{2,1,0:T(8,128)(2,1)} %param.9, f32[3072]{0:T(1024)S(1)} %bitcast.154, f32[128]{0:T(128)S(1)} %add_rsqrt_fusion), kind=kLoop, calls=%fused_computation.40 | loop fusion | flops 3142528 | bytes 1598464 | tf_op jit(solution)/shard_map/reduce_sum | solution.py:187
  125.5 8.6 %psum.14 = f32[1,3072]{1,0:T(1,128)} all-reduce(f32[1,3072]{1,0:T(1,128)S(1)} %bitcast.156), channel_id=1, replica_groups=mesh['rep'=16,'tp'=2] {'tp'}, use_global_device_ids=true, to_apply=%region_6.7 | all-reduce | flops 3072 | bytes 24576 | tf_op jit(solution)/shard_map/psum | solution.py:181
  134.1 2.7 %fusion.49 = bf16[1,128,3072]{2,1,0:T(8,128)(2,1)} fusion(bf16[128,3072]{1,0:T(8,128)(2,1)} %reduce-scatter.2.cloned.1.call-done, bf16[1,128,3072]{2,1,0:T(8,128)(2,1)} %param.9, f32[128]{0:T(128)S(1)} %broadcast_multiply_fusion.1, f32[3072]{0:T(1024)S(1)} %bitcast.155, f32[128]{0:T(128)S(1)} %add_rsqrt_fusion), kind=kLoop, calls=%fused_computation.71 | loop fusion | flops 3145728 | bytes 2372608 | tf_op jit(solution)/shard_map/broadcast_in_dim | solution.py:200
  (35 shorter events, 0.1 us)
Async XLA Ops:
  8.0 36.3 %copy-start = (bf16[1,3072,512]{2,1,0:T(8,128)(2,1)S(1)}, bf16[1,3072,512]{2,1,0:T(8,128)(2,1)}, u32[]{:S(2)}) copy-start(bf16[1,3072,512]{2,1,0:T(8,128)(2,1)} %param.13) | copy-start | bytes 9437188
  8.0 6.9 %copy-start.20 = (bf16[1,64,3072]{2,1,0:T(8,128)(2,1)S(1)}, bf16[1,64,3072]{2,1,0:T(8,128)(2,1)}, u32[]{:S(2)}) copy-start(bf16[1,64,3072]{2,1,0:T(8,128)(2,1)} %param.17) | copy-start | bytes 1179652
  8.0 101.0 %all-reduce.2.cloned.1.call-start = ((), (), s32[]{:S(2)}) async-start(), calls=%async_computation.2 | async-start | bytes 1572864 | tf_op jit(solution)/shard_map/psum | solution.py:192
  8.1 6.8 %copy-start.9 = (f32[64,3072]{1,0:T(8,128)S(1)}, f32[64,3072]{1,0:T(8,128)}, u32[]{:S(2)}) copy-start(f32[64,3072]{1,0:T(8,128)} %param.15) | copy-start | bytes 2359300
  11.9 20.8 %collective-permute-start = (bf16[128,3072]{1,0:T(8,128)(2,1)}, bf16[128,3072]{1,0:T(8,128)(2,1)}, u32[]{:S(2)}, u32[]{:S(2)}) collective-permute-start(bf16[128,3072]{1,0:T(8,128)(2,1)} %fusion.22), channel_id=1, source_target_pairs={{0,1},{1,0},{2,3},{3,2},{4,5},{5,4},{6,7},{7,6},{8,9},{9,8},{10,11... | collective-permute-start | bytes 2359304 | tf_op jit(solution)/shard_map/ppermute | solution.py:108
  15.9 107.7 %reduce-scatter.2.cloned.1.call-start = ((), (), s32[]{:S(2)}) async-start(), calls=%async_computation.1 | async-start | bytes 2359296 | tf_op jit(solution)/shard_map/reduce_scatter | solution.py:172
  35.8 8.5 %copy-start.1 = (bf16[256,3072]{1,0:T(8,128)(2,1)}, bf16[256,3072]{1,0:T(8,128)(2,1)S(1)}, u32[]{:S(2)}) copy-start(bf16[256,3072]{1,0:T(8,128)(2,1)S(1)} %fusion.28) | copy-start | bytes 4718596
  35.9 6.4 %copy-start.8 = (bf16[512,3072]{1,0:T(8,128)(2,1)S(1)}, bf16[512,3072]{1,0:T(8,128)(2,1)}, u32[]{:S(2)}) copy-start(bf16[512,3072]{1,0:T(8,128)(2,1)} %copy.35) | copy-start | bytes 9437188
  41.1 2.2 %copy-start.7 = (f32[256,8,128]{0,2,1:T(8,128)}, f32[256,8,128]{0,2,1:T(8,128)S(1)}, u32[]{:S(2)}) copy-start(f32[256,8,128]{0,2,1:T(8,128)S(1)} %fusion.29) | copy-start | bytes 3145732
  43.3 1.0 copy-start.10
  47.8 2.7 %copy-start.11 = (f32[256,4,128]{0,2,1:T(8,128)S(1)}, f32[256,4,128]{0,2,1:T(8,128)}, u32[]{:S(2)}) copy-start(f32[256,4,128]{0,2,1:T(8,128)} %copy-done.10) | copy-start | bytes 1572868
  47.8 2.7 %copy-start.15 = (f32[256,4,64]{0,2,1:T(8,128)S(1)}, f32[256,4,64]{0,2,1:T(8,128)}, u32[]{:S(2)}) copy-start(f32[256,4,64]{0,2,1:T(8,128)} %get-tuple-element.43) | copy-start | bytes 786436
  47.8 2.7 %copy-start.16 = (f32[256,4,64]{0,2,1:T(8,128)S(1)}, f32[256,4,64]{0,2,1:T(8,128)}, u32[]{:S(2)}) copy-start(f32[256,4,64]{0,2,1:T(8,128)} %get-tuple-element.44) | copy-start | bytes 786436
  47.8 3.5 %copy-start.12 = (bf16[1,256,1024]{1,2,0:T(8,128)(2,1)S(1)}, bf16[1,256,1024]{1,2,0:T(8,128)(2,1)}, u32[]{:S(2)}) copy-start(bf16[1,256,1024]{1,2,0:T(8,128)(2,1)} %copy.41) | copy-start | bytes 1572868
  47.8 3.5 %copy-start.17 = (bf16[256,4,128]{2,1,0:T(4,128)(2,1)S(1)}, bf16[256,4,128]{2,1,0:T(4,128)(2,1)}, u32[]{:S(2)}) copy-start(bf16[256,4,128]{2,1,0:T(4,128)(2,1)} %reshape.115) | copy-start | bytes 786436
  67.0 2.4 %copy-start.18 = (f32[256,4,128]{0,2,1:T(8,128)S(1)}, f32[256,4,128]{0,2,1:T(8,128)}, u32[]{:S(2)}) copy-start(f32[256,4,128]{0,2,1:T(8,128)} %get-tuple-element.49) | copy-start | bytes 1572868
  67.0 2.4 %copy-start.4 = (f32[4,128,2,256]{3,1,2,0:T(8,128)S(1)}, f32[4,128,2,256]{3,1,2,0:T(8,128)}, u32[]{:S(2)}) copy-start(f32[4,128,2,256]{3,1,2,0:T(8,128)} %fusion.47) | copy-start | bytes 3145732
  67.0 3.7 %slice-start = ((s8[6291456]{0:T(1024)(128)(4,1)}), s8[4194304]{0:T(1024)(128)(4,1)S(1)}, s32[]{:S(2)}) async-start(s8[6291456]{0:T(1024)(128)(4,1)} %bitcast.139), calls=%async_computation.3 | async-start | bytes 8388608
  69.3 5.8 %copy-start.13 = (bf16[4,256,128]{1,2,0:T(8,128)(2,1)}, bf16[4,256,128]{1,2,0:T(8,128)(2,1)S(1)}, u32[]{:S(2)}) copy-start(bf16[4,256,128]{1,2,0:T(8,128)(2,1)S(1)} %fusion.36) | copy-start | bytes 786436
  69.4 2.5 %slice-start.1 = ((s8[6291456]{0:T(1024)(128)(4,1)}), s8[2097152]{0:T(1024)(128)(4,1)S(1)}, s32[]{:S(2)}) async-start(s8[6291456]{0:T(1024)(128)(4,1)} %bitcast.139), calls=%async_computation.4 | async-start | bytes 4194304
  71.8 1.9 %copy-start.19 = (f32[256,4,128]{0,2,1:T(8,128)S(1)}, f32[256,4,128]{0,2,1:T(8,128)}, u32[]{:S(2)}) copy-start(f32[256,4,128]{0,2,1:T(8,128)} %get-tuple-element.50) | copy-start | bytes 1572868
  71.8 2.1 %copy-start.3 = (bf16[1,3072,512]{2,1,0:T(8,128)(2,1)S(1)}, bf16[1,3072,512]{2,1,0:T(8,128)(2,1)}, u32[]{:S(2)}) copy-start(bf16[1,3072,512]{2,1,0:T(8,128)(2,1)} %param.12) | copy-start | bytes 9437188
  109.1 3.1 %copy-start.5 = (f32[4,128,2,256]{3,1,2,0:T(8,128)S(1)}, f32[4,128,2,256]{3,1,2,0:T(8,128)}, u32[]{:S(2)}) copy-start(f32[4,128,2,256]{3,1,2,0:T(8,128)} %fusion.47) | copy-start | bytes 3145732
  109.1 3.1 %copy-start.6 = (f32[256,8,128]{0,2,1:T(8,128)S(1)}, f32[256,8,128]{0,2,1:T(8,128)}, u32[]{:S(2)}) copy-start(f32[256,8,128]{0,2,1:T(8,128)} %get-tuple-element.36) | copy-start | bytes 3145732
  112.2 1.4 copy-start.2
  112.2 1.4 copy-start.14
  119.0 4.6 %copy-start.21 = (f32[1,3072]{1,0:T(1,128)S(1)}, f32[1,3072]{1,0:T(1,128)}, u32[]{:S(2)}) copy-start(f32[1,3072]{1,0:T(1,128)} %param.10) | copy-start | bytes 36868
Sparse Core Ops, SparseCore 0:
  16.0 93.0 all-reduce.1
Sparse Core Ops, SparseCore 1:
  77.5 27.5 reduce-scatter.1
